TPU v7x, 128 devices: a whole 4x4x4 slice. The times are simulated.
128 devices in a mesh: data: 1, fsdp: 2 (over core), ep: 64 (over z, y, x).
Axes of the slice: x: 4, y: 4, z: 4, core: 2. Of those that a mesh axis runs over, the one named last changes fastest.
Arguments:
- x_in: bfloat16 [128, 384, 2048], P(('data', 'fsdp', 'ep'))
- w_qkv: bfloat16 [2048, 6144], P('fsdp')
- w_out: bfloat16 [2048, 2048], P('fsdp')
- w_gate: bfloat16 [64, 2048, 1408], P('ep', 'fsdp')
- w_up: bfloat16 [64, 2048, 1408], P('ep', 'fsdp')
- w_down: bfloat16 [64, 1408, 2048], P('ep', None, 'fsdp')
- ws_gate: bfloat16 [2048, 2816], P('fsdp')
- ws_up: bfloat16 [2048, 2816], P('fsdp')
- ws_down: bfloat16 [2816, 2048], P(None, 'fsdp')
- expert_ids: int32 [128, 384, 6], P(('data', 'fsdp', 'ep'))
- slot_ids: int32 [128, 384, 6], P(('data', 'fsdp', 'ep'))
- gate_vals: bfloat16 [128, 384, 6], P(('data', 'fsdp', 'ep'))
Outputs:
- output: bfloat16 [128, 384, 2048], P(('data', 'fsdp', 'ep'))
All inputs are finite; a program needn't handle non-finite values.
Results may differ from a plain program's by a relative error of at most 0.00961563.
Values are sent between devices in bfloat16 or wider.
A program may use at most 1 GiB of HBM per device.

v0:
```python
import functools

import jax
import jax.numpy as jnp
import numpy as np
from jax import lax
from jax.experimental import pallas as pl
from jax.experimental.pallas import tpu as pltpu
from jax.sharding import PartitionSpec as P

HEAD_DIM = 128
ROPE_BASE = 10000.0
EPSILON = 1e-6
RING = 4
BLOCK = 8
TURNS = 3
WIDE = 256
MESH = pl.DeviceIdType.MESH
STRIDES = (RING * RING, RING, 1)


def rms_norm(values):
    vals_f32 = values.astype(jnp.float32)
    mean_sq = jnp.mean(vals_f32 * vals_f32, axis=-1, keepdims=True)
    return (vals_f32 * lax.rsqrt(mean_sq + EPSILON)).astype(jnp.bfloat16)


def rotary_tables(seq_len):
    half_dim = HEAD_DIM // 2
    inv_freq = (ROPE_BASE ** (-np.arange(half_dim) * (2.0 / HEAD_DIM))).astype(np.float32)
    angles = (np.arange(seq_len, dtype=np.float32)[:, None] * inv_freq[None, :]).astype(np.float64)
    cos_tab, sin_tab = np.cos(angles), np.sin(angles)
    return (np.concatenate([cos_tab, cos_tab], axis=1).astype(np.float32), np.concatenate([-sin_tab, sin_tab], axis=1).astype(np.float32))


def dot32(left, right):
    return jnp.dot(left, right, preferred_element_type=jnp.float32)


def norm_rows(src_ref, dst_ref, group=48):
    def step(g, carry):
        at = pl.ds(pl.multiple_of(g * group, group), group)
        dst_ref[at, :] = rms_norm(src_ref[at, :])
        return carry

    lax.fori_loop(0, src_ref.shape[0] // group, step, 0)


def attention_kernel(x_ref, cos_ref, sin_ref, qkv_hbm, out_hbm, hidden_ref, normed_ref,
                     a_ref, o_ref, own_ref, far_ref, wo_own, wo_far, own_sem, send_sem, recv_sem, wo_sem):
    fs = lax.axis_index("fsdp")
    partner = {"fsdp": 1 - fs}
    seq_len, width = x_ref.shape
    half = width // 2
    n_chunks = width // WIDE
    barrier = pltpu.get_barrier_semaphore()
    pl.semaphore_signal(barrier, inc=1, device_id=partner, device_id_type=MESH)
    pl.semaphore_wait(barrier, 1)
    for c in range(n_chunks):
        for t in range(3):
            cols = qkv_hbm.at[:, pl.ds(t * width + c * WIDE, WIDE)]
            pltpu.make_async_remote_copy(src_ref=cols, dst_ref=far_ref.at[c, t], send_sem=send_sem.at[c], recv_sem=recv_sem.at[c],
                                         device_id=partner, device_id_type=MESH).start()
            pltpu.make_async_copy(cols, own_ref.at[c, t], own_sem.at[c]).start()
    wo_push = pltpu.make_async_remote_copy(src_ref=out_hbm, dst_ref=wo_far, send_sem=send_sem.at[n_chunks], recv_sem=recv_sem.at[n_chunks],
                                           device_id=partner, device_id_type=MESH)
    wo_push.start()
    wo_load = pltpu.make_async_copy(out_hbm, wo_own, wo_sem)
    wo_load.start()
    norm_rows(x_ref, a_ref)

    def own(side):
        return pl.ds(pl.multiple_of(lax.rem(fs + side, 2) * half, half), half)

    def chunk_step(c, carry):
        pltpu.make_async_copy(own_ref.at[c], own_ref.at[c], own_sem.at[c]).wait()
        pltpu.make_async_copy(far_ref.at[c], far_ref.at[c], recv_sem.at[c]).wait()
        left, right = a_ref[:, own(0)], a_ref[:, own(1)]
        q, k, v = [(dot32(left, own_ref[c, t]) + dot32(right, far_ref[c, t])).astype(jnp.bfloat16) for t in range(3)]

        def rotate(vals):
            wide = vals.astype(jnp.float32)
            return (wide * cos_ref[...] + pltpu.roll(wide, HEAD_DIM // 2, 1) * sin_ref[...]).astype(jnp.bfloat16)

        heads = []
        for j in range(WIDE // HEAD_DIM):
            cols = slice(j * HEAD_DIM, (j + 1) * HEAD_DIM)
            query, key, value = rotate(q[:, cols]), rotate(k[:, cols]), v[:, cols]
            parts = []
            for i in range(seq_len // 128):
                span = (i + 1) * 128
                scores = lax.dot_general(query[i * 128:span], key[:span], (((1,), (1,)), ((), ())), preferred_element_type=jnp.float32) * (HEAD_DIM ** -0.5)
                row_at = lax.broadcasted_iota(jnp.int32, (128, span), 0) + i * 128
                col_at = lax.broadcasted_iota(jnp.int32, (128, span), 1)
                scores = jnp.where(row_at >= col_at, scores, -1e30)
                power = jnp.exp(scores - jnp.max(scores, axis=-1, keepdims=True))
                probs = (power / jnp.sum(power, axis=-1, keepdims=True)).astype(jnp.bfloat16)
                parts.append(dot32(probs, value[:span]).astype(jnp.bfloat16))
            heads.append(jnp.concatenate(parts, axis=0))
        o_ref[:, pl.ds(pl.multiple_of(c * WIDE, WIDE), WIDE)] = jnp.concatenate(heads, axis=1)
        return carry

    lax.fori_loop(0, n_chunks, chunk_step, 0)
    wo_load.wait()
    wo_push.wait_recv()

    def out_step(n, carry):
        cols = pl.ds(pl.multiple_of(n * WIDE, WIDE), WIDE)
        mixed = dot32(o_ref[:, own(0)], wo_own[:, cols]) + dot32(o_ref[:, own(1)], wo_far[:, cols])
        hidden_ref[:, cols] = (x_ref[:, cols].astype(jnp.float32) + mixed).astype(jnp.bfloat16)
        return carry

    lax.fori_loop(0, n_chunks, out_step, 0)
    norm_rows(hidden_ref, normed_ref)
    for c in range(n_chunks):
        pltpu.make_async_copy(far_ref.at[c], far_ref.at[c], send_sem.at[c]).wait()
    wo_push.wait_send()


def attention(x_rows, w_qkv, w_out):
    seq_len, width = x_rows.shape
    half, n_chunks = width // 2, width // WIDE
    anywhere = pl.BlockSpec(memory_space=pl.ANY)
    vmem = pl.BlockSpec(memory_space=pltpu.VMEM)
    rows = jax.ShapeDtypeStruct((seq_len, width), jnp.bfloat16)
    sems = pltpu.SemaphoreType.DMA
    cos_tab, sin_tab = rotary_tables(seq_len)
    return pl.pallas_call(
        attention_kernel,
        out_shape=(rows, rows),
        in_specs=[vmem] * 3 + [anywhere] * 2,
        out_specs=(vmem, vmem),
        scratch_shapes=[
            pltpu.VMEM((seq_len, width), jnp.bfloat16),
            pltpu.VMEM((seq_len, width), jnp.bfloat16),
            pltpu.VMEM((n_chunks, 3, half, WIDE), jnp.bfloat16),
            pltpu.VMEM((n_chunks, 3, half, WIDE), jnp.bfloat16),
            pltpu.VMEM(w_out.shape, jnp.bfloat16),
            pltpu.VMEM(w_out.shape, jnp.bfloat16),
            sems((n_chunks,)), sems((n_chunks + 1,)), sems((n_chunks + 1,)), sems(()),
        ],
        compiler_params=pltpu.CompilerParams(collective_id=1, has_side_effects=True, vmem_limit_bytes=56 * 1024 * 1024),
        cost_estimate=pl.CostEstimate(flops=20_000_000_000, bytes_accessed=40_000_000, transcendentals=3_000_000),
        name="attention",
    )(x_rows, jnp.asarray(cos_tab), jnp.asarray(sin_tab), w_qkv, w_out)


def capacity_for(n_tokens, top_k, n_experts):
    return ((5 * n_tokens * top_k) // (4 * n_experts) + 7) // 8 * 8


def ring_peer(me, axis, offset):
    stride = RING * RING - 12 * axis + 9 * (axis * (axis - 1) // 2)
    place = lax.rem(me // stride, RING)
    return me + (lax.rem(place + offset + RING, RING) - place) * stride


class Exchange:
    def __init__(self, me, axes, sign, unit, buffers, send, recv):
        self.me, self.axes, self.sign = me, axes, sign
        self.first, self.second, self.third, self.last = [ref.at[unit] for ref in buffers]
        self.send, self.recv = send.at[unit], recv.at[unit]

    def push(self, phase, step, pairs):
        peer = ring_peer(self.me, self.axes[phase], self.sign * step)
        for src, dst in pairs:
            pltpu.make_async_remote_copy(src_ref=src, dst_ref=dst, send_sem=self.send.at[phase], recv_sem=self.recv.at[phase],
                                         device_id={"ep": peer}, device_id_type=MESH).start()

    def start(self, phase):
        for d in (1, 3, 2):
            if phase == 0:
                pairs = [(self.first.at[d], self.second.at[:, :, d - 1])]
            elif phase == 1:
                pairs = [(self.first.at[0, d], self.third.at[:, d - 1, 0]), (self.second.at[d], self.third.at[:, d - 1, pl.ds(1, 3)])]
            else:
                pairs = [(self.first.at[0, 0, d], self.last.at[d - 1, 0, 0]), (self.second.at[0, d], self.last.at[d - 1, 0, pl.ds(1, 3)]),
                         (self.third.at[d], self.last.at[d - 1, pl.ds(1, 3)])]
            self.push(phase, d, pairs)

    def landing(self, phase):
        return (self.second, self.third, self.last)[phase]

    def wait_recv(self, phase):
        whole = self.landing(phase)
        pltpu.make_async_copy(whole, whole, self.recv.at[phase]).wait()

    def wait_send(self, phase):
        whole = self.landing(phase)
        pltpu.make_async_copy(whole, whole, self.send.at[phase]).wait()

    def kept(self):
        return [(self.third.at[0], (0, pl.ds(1, 3))), (self.second.at[0, 0], (0, 0, pl.ds(1, 3))), (self.first.at[0, 0, 0], (0, 0, 0))]


def moe_kernel(n_units, normed_ref, hidden_ref, place_ref, weight_ref,
               gate_a, up_a, down_a, sgate_a, sup_a, sdown_a, sum_ref,
               sgate_b, sup_b, sdown_b, rows_hbm, out1, out2, out3, made_hbm, back1, back2, back3,
               ga, gb, ua, ub, da, db, sin_ref, sdn_ref, x_ref, act_ref, y_ref, total_ref, mix_ref, pick_ref,
               w_sem, pair_send, pair_recv, far_send, far_recv, s_sem, x_sem, y_sem, go_send, go_recv, come_send, come_recv):
    me = lax.axis_index("ep")
    fs = lax.axis_index("fsdp")
    barrier = pltpu.get_barrier_semaphore()
    for axis in range(3):
        for d in range(1, RING):
            pl.semaphore_signal(barrier, inc=1, device_id={"ep": ring_peer(me, axis, d)}, device_id_type=MESH)
    partner = {"fsdp": 1 - fs}
    pl.semaphore_signal(barrier, inc=1, device_id=partner, device_id_type=MESH)
    pl.semaphore_wait(barrier, 3 * (RING - 1) + 1)

    half = ga.shape[0]
    inner = ga.shape[1]
    rows = RING ** 3 * BLOCK
    n_tokens = normed_ref.shape[0]
    top_k = place_ref.shape[0]

    def go(u):
        return Exchange(me, [lax.rem(u + k, 3) for k in range(3)], 1, u, (rows_hbm, out1, out2, out3), go_send, go_recv)

    def come(u):
        return Exchange(me, [lax.rem(u + 2 - k, 3) for k in range(3)], -1, u, (made_hbm, back1, back2, back3), come_send, come_recv)

    def advance(exchange, phase):
        exchange.wait_recv(phase)
        exchange.start(phase + 1)

    def each(low, high, step):
        def body(u, carry):
            step(u)
            return carry

        lax.fori_loop(low, high, body, 0)

    def own(side):
        return pl.ds(pl.multiple_of(lax.rem(fs + side, 2) * half, half), half)

    def own_block(side, n):
        return pl.ds(pl.multiple_of(lax.rem(fs + side, 2) * half + n * WIDE, WIDE), WIDE)

    def block_at(n):
        return pl.ds(pl.multiple_of(n * WIDE, WIDE), WIDE)

    def shared_copies(n, slot):
        pairs = [(src, sin_ref.at[slot, k]) for k, src in enumerate((sgate_a.at[:, block_at(n)], sgate_b.at[n], sup_a.at[:, block_at(n)], sup_b.at[n]))]
        pairs += [(src.at[block_at(n)], sdn_ref.at[slot, k]) for k, src in enumerate((sdown_a, sdown_b))]
        return [pltpu.make_async_copy(src, dst, s_sem.at[slot, k]) for k, (src, dst) in enumerate(pairs)]

    def shared_push(n):
        pairs = [(sgate_a.at[:, block_at(n)], sgate_b.at[n]), (sup_a.at[:, block_at(n)], sup_b.at[n]), (sdown_a.at[block_at(n)], sdown_b.at[block_at(n)])]
        return [pltpu.make_async_remote_copy(src_ref=src, dst_ref=dst, send_sem=pair_send.at[k, n], recv_sem=pair_recv.at[k, n],
                                             device_id=partner, device_id_type=MESH) for k, (src, dst) in enumerate(pairs)]

    n_shared = sgate_a.shape[1] // WIDE
    ahead = 3
    for n in range(ahead):
        for copy in shared_push(n):
            copy.start()

    def pick(u):
        slot = lax.rem(u, 2)
        for c in range(rows // 128):
            at = lax.broadcasted_iota(jnp.int32, (128, n_tokens), 0) + (u * rows + c * 128)
            part = jnp.zeros((128, n_tokens), jnp.float32)
            for k in range(top_k):
                part += jnp.where(place_ref[k:k + 1, :] == at, 1.0, 0.0)
            pick_ref[c * 128:(c + 1) * 128, :] = part.astype(jnp.bfloat16)
        x2 = x_ref.at[slot].reshape(rows, 2 * half)

        def pick_step(n, carry):
            x2[:, block_at(n)] = dot32(pick_ref[...], normed_ref[:, block_at(n)]).astype(jnp.bfloat16)
            return carry

        lax.fori_loop(0, 2 * half // WIDE, pick_step, 0)
        copy = pltpu.make_async_copy(x_ref.at[slot], rows_hbm.at[u], y_sem.at[slot])
        copy.start()
        copy.wait()
        go(u).start(0)

    each(0, n_units, pick)
    weights = [pltpu.make_async_copy(src, dst, w_sem.at[n]) for n, (src, dst) in enumerate(((gate_a, ga), (up_a, ua), (down_a, da)))]
    far_weights = [pltpu.make_async_remote_copy(src_ref=src, dst_ref=dst, send_sem=far_send.at[n], recv_sem=far_recv.at[n], device_id=partner, device_id_type=MESH)
                   for n, (src, dst) in enumerate(((gate_a, gb), (up_a, ub), (down_a, db)))]
    for copy in weights:
        copy.start()
    for copy in shared_push(0):
        copy.wait_recv()
    for copy in shared_copies(0, 0):
        copy.start()
    total_ref[...] = hidden_ref[...].astype(jnp.float32)

    def shared_step(n, carry):
        slot = lax.rem(n, 2)
        for copy in shared_copies(n, slot):
            copy.wait()

        @pl.when(n == 4)
        def _():
            each(0, TURNS, lambda u: advance(go(u), 0))

        @pl.when(n + ahead < n_shared)
        def _():
            for copy in shared_push(n + ahead):
                copy.start()

        @pl.when(n + 1 < n_shared)
        def _():
            for copy in shared_push(n + 1):
                copy.wait_recv()
            for copy in shared_copies(n + 1, 1 - slot):
                copy.start()

        left, right = normed_ref[:, own(0)], normed_ref[:, own(1)]
        gate = dot32(left, sin_ref[slot, 0]) + dot32(right, sin_ref[slot, 1])
        up = dot32(left, sin_ref[slot, 2]) + dot32(right, sin_ref[slot, 3])
        act_ref[pl.ds(0, n_tokens), pl.ds(0, WIDE)] = (jax.nn.silu(gate) * up).astype(jnp.bfloat16)

        def shared_down(m, c):
            for side in range(2):
                total_ref[:, own_block(side, m)] += dot32(act_ref[pl.ds(0, n_tokens), pl.ds(0, WIDE)], sdn_ref[slot, side, :, block_at(m)])
            return c

        lax.fori_loop(0, half // WIDE, shared_down, 0)
        return carry

    lax.fori_loop(0, n_shared, shared_step, 0)
    for copy in far_weights:
        copy.start()

    each(TURNS, n_units, lambda u: advance(go(u), 0))
    each(0, n_units, lambda u: advance(go(u), 1))
    for copy in weights:
        copy.wait()
    for copy in far_weights:
        copy.wait_recv()

    def loads(exchange, slot):
        pieces = [(exchange.last, (pl.ds(1, 3),))] + exchange.kept()
        return [pltpu.make_async_copy(src, x_ref.at[(slot, *place)], x_sem.at[slot, n]) for n, (src, place) in enumerate(pieces)]

    def fetch(exchange, slot):
        exchange.wait_recv(2)
        for copy in loads(exchange, slot):
            copy.start()

    def expert(slot):
        x2 = x_ref.at[slot].reshape(rows, 2 * half)
        y2 = y_ref.at[slot].reshape(rows, 2 * half)

        def inner_block(cols):
            gate = dot32(x2[:, own(0)], ga[:, cols]) + dot32(x2[:, own(1)], gb[:, cols])
            up = dot32(x2[:, own(0)], ua[:, cols]) + dot32(x2[:, own(1)], ub[:, cols])
            act_ref[:, cols] = (jax.nn.silu(gate) * up).astype(jnp.bfloat16)

        def inner_step(n, carry):
            inner_block(block_at(n))
            return carry

        whole = inner // WIDE
        lax.fori_loop(0, whole, inner_step, 0)
        if inner % WIDE:
            inner_block(pl.ds(whole * WIDE, inner % WIDE))

        def down_step(n, carry):
            for side, weight in enumerate((da, db)):
                y2[:, own_block(side, n)] = dot32(act_ref[...], weight[:, block_at(n)]).astype(jnp.bfloat16)
            return carry

        lax.fori_loop(0, half // WIDE, down_step, 0)

    fetch(go(0), 0)

    def expert_unit(u):
        slot = lax.rem(u, 2)
        for copy in loads(go(u), slot):
            copy.wait()

        @pl.when(u + 1 < n_units)
        def _():
            fetch(go(u + 1), 1 - slot)

        expert(slot)
        copy = pltpu.make_async_copy(y_ref.at[slot], made_hbm.at[u], y_sem.at[slot])
        copy.start()
        copy.wait()
        come(u).start(0)

        @pl.when(u >= TURNS)
        def _():
            advance(come(u - TURNS), 0)

    each(0, n_units, expert_unit)
    each(n_units - TURNS, n_units, lambda u: advance(come(u), 0))
    each(0, n_units, lambda u: advance(come(u), 1))
    fetch(come(0), 0)

    def mix(u):
        slot = lax.rem(u, 2)
        for c in range(rows // 128):
            at = lax.broadcasted_iota(jnp.int32, (128, n_tokens), 0) + (u * rows + c * 128)
            part = jnp.zeros((128, n_tokens), jnp.float32)
            for k in range(top_k):
                part += jnp.where(place_ref[k:k + 1, :] == at, weight_ref[k:k + 1, :], 0.0)
            mix_ref[:, c * 128:(c + 1) * 128] = part.T.astype(jnp.bfloat16)
        for copy in loads(come(u), slot):
            copy.wait()

        @pl.when(u + 1 < n_units)
        def _():
            fetch(come(u + 1), 1 - slot)

        x2 = x_ref.at[slot].reshape(rows, 2 * half)

        def mix_step(n, carry):
            total_ref[:, block_at(n)] += dot32(mix_ref[...], x2[:, block_at(n)])
            return carry

        lax.fori_loop(0, 2 * half // WIDE, mix_step, 0)

    each(0, n_units, mix)
    sum_ref[...] = total_ref[...].astype(jnp.bfloat16)
    for copy in far_weights:
        copy.wait_send()

    def pair_done(n, carry):
        for copy in shared_push(n):
            copy.wait_send()
        return carry

    lax.fori_loop(0, n_shared, pair_done, 0)

    def sent(u):
        for phase in range(3):
            go(u).wait_send(phase)
            come(u).wait_send(phase)

    each(0, n_units, sent)


def moe_exchange(n_units, normed, hidden, place, weight, weights, shared):
    n_tokens, width = normed.shape
    anywhere = pl.BlockSpec(memory_space=pl.ANY)
    vmem = pl.BlockSpec(memory_space=pltpu.VMEM)
    inner, n_shared = weights[0].shape[1], shared[0].shape[1] // WIDE

    def blocks(*lead):
        return jax.ShapeDtypeStruct((n_units, *lead, BLOCK, width), jnp.bfloat16)

    cube = (RING, RING, RING, BLOCK, width)
    steps = [blocks(4, 4, 3), blocks(4, 3, 4), blocks(3, 4, 4)]
    wide_block = jax.ShapeDtypeStruct((n_shared, width // 2, WIDE), jnp.bfloat16)
    far = [wide_block, wide_block, jax.ShapeDtypeStruct(shared[2].shape, jnp.bfloat16)]
    outs = [jax.ShapeDtypeStruct((n_tokens, width), jnp.bfloat16)] + far + [blocks(4, 4, 4)] + steps + [blocks(4, 4, 4)] + steps
    sems = pltpu.SemaphoreType.DMA
    return pl.pallas_call(
        functools.partial(moe_kernel, n_units),
        out_shape=tuple(outs),
        in_specs=[vmem] * 4 + [anywhere] * 6,
        out_specs=(vmem,) + (anywhere,) * 11,
        scratch_shapes=[pltpu.VMEM(w.shape, jnp.bfloat16) for w in weights for _ in range(2)] + [
            pltpu.VMEM((2, 4, width // 2, WIDE), jnp.bfloat16),
            pltpu.VMEM((2, 2, WIDE, width // 2), jnp.bfloat16),
            pltpu.VMEM((2, *cube), jnp.bfloat16),
            pltpu.VMEM((RING ** 3 * BLOCK, inner), jnp.bfloat16),
            pltpu.VMEM((2, *cube), jnp.bfloat16),
            pltpu.VMEM((n_tokens, width), jnp.float32),
            pltpu.VMEM((n_tokens, RING ** 3 * BLOCK), jnp.bfloat16),
            pltpu.VMEM((RING ** 3 * BLOCK, n_tokens), jnp.bfloat16),
            sems((3,)), sems((3, n_shared)), sems((3, n_shared)), sems((3,)), sems((3,)), sems((2, 6)), sems((2, 4)), sems((2,)),
            sems((n_units, 3)), sems((n_units, 3)), sems((n_units, 3)), sems((n_units, 3)),
        ],
        compiler_params=pltpu.CompilerParams(collective_id=0, has_side_effects=True, vmem_limit_bytes=60 * 1024 * 1024),
        cost_estimate=pl.CostEstimate(flops=250_000_000_000, bytes_accessed=100_000_000, transcendentals=0),
        name="moe_exchange",
    )(normed, hidden, place, weight, *weights, *shared)[0]


def solution(mesh):
    n_ep = mesh.shape["ep"]
    tok_spec = P(("data", "fsdp", "ep"))
    row_spec = P("fsdp", None)

    def local_step(x_in, w_qkv, w_out, w_gate, w_up, w_down, ws_gate, ws_up, ws_down, expert_ids, slot_ids, gate_vals):
        n_batch, seq_len, model_dim = x_in.shape
        n_tokens = n_batch * seq_len
        top_k = expert_ids.shape[-1]
        n_experts = w_gate.shape[0] * n_ep
        capacity = capacity_for(n_tokens, top_k, n_experts)
        ids_flat = expert_ids.reshape(n_tokens, top_k).T
        slots_flat = slot_ids.reshape(n_tokens, top_k).T
        me = lax.axis_index("ep")
        rel = [lax.rem(ids_flat // s - me // s + n_ep, RING) for s in STRIDES]
        unit, within = slots_flat // BLOCK, slots_flat % BLOCK
        turn = unit % TURNS
        place = jnp.zeros_like(slots_flat)
        for r in range(TURNS):
            order = [rel[(r + k) % 3] for k in range(3)]
            place = jnp.where(turn == r, (order[0] * RING + order[1]) * RING + order[2], place)
        row_of = jnp.where(slots_flat >= 0, (unit * n_experts + place) * BLOCK + within, -1)
        gates = gate_vals.reshape(n_tokens, top_k).T.astype(jnp.float32)
        hidden, normed = attention(x_in.reshape(n_tokens, model_dim), w_qkv, w_out)
        summed = moe_exchange(capacity // BLOCK, normed, hidden, row_of, gates, (w_gate[0], w_up[0], w_down[0]), (ws_gate, ws_up, ws_down))
        return summed.reshape(n_batch, seq_len, model_dim)

    return jax.shard_map(local_step, mesh=mesh, in_specs=(tok_spec, row_spec, row_spec, P("ep", "fsdp", None), P("ep", "fsdp", None), P("ep", None, "fsdp"), row_spec, row_spec, P(None, "fsdp"), tok_spec, tok_spec, tok_spec), out_specs=tok_spec, check_vma=False)
```

profile of v0, /device:TPU:0, one launch (start us, length us, event | category | flops | bytes accessed | tf_op | source)
XLA Modules:
  0.0 377.8 jit_solution(1515358190844284212)
XLA Ops:
  0.0 1.4 fusion.10.place_ref
  1.4 1.3 convert_bitcast_fusion.weight_ref
  2.7 41.5 %attention.1 = (bf16[384,2048]{1,0:T(8,128)(2,1)}, bf16[384,2048]{1,0:T(8,128)(2,1)}) custom-call(bf16[384,2048]{1,0:T(8,128)(2,1)} %bitcast.64, f32[384,128]{1,0:T(8,128)} %constant.110.clone.cos_ref, f32[384,128]{1,0:T(8,128)} %constant.111.clone.sin_ref, bf16[1024,6144]{1,0:T(8,128)(2,1)} %qkv_hbm.1, bf16[1024,2048]{1,0:T(8,128)(2,1)} %out_hbm.1), custom_call_target="tpu_custom_call" | custom-call | flops 20000000000 | bytes 40000000 | tf_op jit(solution)/shard_map/attention/pallas_call | solution.py:128
  44.2 330.9 %moe_exchange.1 = (bf16[384,2048]{1,0:T(8,128)(2,1)}, bf16[11,1024,256]{2,1,0:T(8,128)(2,1)}, bf16[11,1024,256]{2,1,0:T(8,128)(2,1)}, bf16[2816,1024]{1,0:T(8,12...) custom-call(bf16[384,2048]{1,0:T(8,128)(2,1)} %get-tuple-element.8.n, ...), custom_call_target="tpu_custom_call" | custom-call | flops 249999998976 | bytes 100000000 | tf_op jit(solution)/shard_map/moe_exchange/pallas_call | solution.py:454
  375.1 2.7 copy.62
where the time goes:
time: 378 us
  Pallas kernels  372 us (98%)
    pallas_call x1, Pallas kernels, moe_exchange(): pl.pallas_call(functools.partial(moe_kernel, n_units), out_shape=tuple(ou...  331 us
    pallas_call x1, Pallas kernels, attention(): pl.pallas_call(attention_kernel, out_shape=(rows, rows), in_specs=[vmem]...  41.5 us

commit v1 on v0

--- a/solution.py
+++ b/solution.py
@@ -161,33 +161,36 @@
         self.first, self.second, self.third, self.last = [ref.at[unit] for ref in buffers]
         self.send, self.recv = send.at[unit], recv.at[unit]
 
-    def push(self, phase, step, pairs):
-        peer = ring_peer(self.me, self.axes[phase], self.sign * step)
+    def push(self, phase, d):
+        peer = ring_peer(self.me, self.axes[phase], self.sign * d)
+        if phase == 0:
+            pairs = [(self.first.at[d], self.second.at[:, :, d - 1])]
+        elif phase == 1:
+            pairs = [(self.first.at[0, d], self.third.at[:, d - 1, 0]), (self.second.at[d], self.third.at[:, d - 1, pl.ds(1, 3)])]
+        else:
+            pairs = [(self.first.at[0, 0, d], self.last.at[d - 1, 0, 0]), (self.second.at[0, d], self.last.at[d - 1, 0, pl.ds(1, 3)]),
+                     (self.third.at[d], self.last.at[d - 1, pl.ds(1, 3)])]
+        sem = phase if phase < 2 else 1 + d
         for src, dst in pairs:
-            pltpu.make_async_remote_copy(src_ref=src, dst_ref=dst, send_sem=self.send.at[phase], recv_sem=self.recv.at[phase],
+            pltpu.make_async_remote_copy(src_ref=src, dst_ref=dst, send_sem=self.send.at[sem], recv_sem=self.recv.at[sem],
                                          device_id={"ep": peer}, device_id_type=MESH).start()
 
     def start(self, phase):
         for d in (1, 3, 2):
-            if phase == 0:
-                pairs = [(self.first.at[d], self.second.at[:, :, d - 1])]
-            elif phase == 1:
-                pairs = [(self.first.at[0, d], self.third.at[:, d - 1, 0]), (self.second.at[d], self.third.at[:, d - 1, pl.ds(1, 3)])]
-            else:
-                pairs = [(self.first.at[0, 0, d], self.last.at[d - 1, 0, 0]), (self.second.at[0, d], self.last.at[d - 1, 0, pl.ds(1, 3)]),
-                         (self.third.at[d], self.last.at[d - 1, pl.ds(1, 3)])]
-            self.push(phase, d, pairs)
-
-    def landing(self, phase):
-        return (self.second, self.third, self.last)[phase]
+            self.push(phase, d)
 
     def wait_recv(self, phase):
-        whole = self.landing(phase)
+        whole = (self.second, self.third)[phase]
         pltpu.make_async_copy(whole, whole, self.recv.at[phase]).wait()
 
-    def wait_send(self, phase):
-        whole = self.landing(phase)
-        pltpu.make_async_copy(whole, whole, self.send.at[phase]).wait()
+    def wait_last(self, d):
+        pltpu.make_async_copy(self.last.at[d - 1], self.last.at[d - 1], self.recv.at[1 + d]).wait()
+
+    def wait_sent(self):
+        for phase, whole in enumerate((self.second, self.third)):
+            pltpu.make_async_copy(whole, whole, self.send.at[phase]).wait()
+        for d in range(1, RING):
+            pltpu.make_async_copy(self.last.at[d - 1], self.last.at[d - 1], self.send.at[1 + d]).wait()
 
     def kept(self):
         return [(self.third.at[0], (0, pl.ds(1, 3))), (self.second.at[0, 0], (0, 0, pl.ds(1, 3))), (self.first.at[0, 0, 0], (0, 0, 0))]
@@ -271,7 +274,7 @@
             return carry
 
         lax.fori_loop(0, 2 * half // WIDE, pick_step, 0)
-        copy = pltpu.make_async_copy(x_ref.at[slot], rows_hbm.at[u], y_sem.at[slot])
+        copy = pltpu.make_async_copy(x_ref.at[slot], rows_hbm.at[u], y_sem.at[slot, 0])
         copy.start()
         copy.wait()
         go(u).start(0)
@@ -327,29 +330,22 @@
         copy.start()
 
     each(TURNS, n_units, lambda u: advance(go(u), 0))
-    each(0, n_units, lambda u: advance(go(u), 1))
+    each(0, TURNS, lambda u: advance(go(u), 1))
     for copy in weights:
         copy.wait()
     for copy in far_weights:
         copy.wait_recv()
 
-    def loads(exchange, slot):
-        pieces = [(exchange.last, (pl.ds(1, 3),))] + exchange.kept()
-        return [pltpu.make_async_copy(src, x_ref.at[(slot, *place)], x_sem.at[slot, n]) for n, (src, place) in enumerate(pieces)]
-
-    def fetch(exchange, slot):
-        exchange.wait_recv(2)
-        for copy in loads(exchange, slot):
-            copy.start()
-
-    def expert(slot):
+    tile = TURNS * RING * RING * BLOCK
+    top = pl.ds(0, tile)
+
+    def inner_part(slot):
         x2 = x_ref.at[slot].reshape(rows, 2 * half)
-        y2 = y_ref.at[slot].reshape(rows, 2 * half)
 
         def inner_block(cols):
-            gate = dot32(x2[:, own(0)], ga[:, cols]) + dot32(x2[:, own(1)], gb[:, cols])
-            up = dot32(x2[:, own(0)], ua[:, cols]) + dot32(x2[:, own(1)], ub[:, cols])
-            act_ref[:, cols] = (jax.nn.silu(gate) * up).astype(jnp.bfloat16)
+            gate = dot32(x2[top, own(0)], ga[:, cols]) + dot32(x2[top, own(1)], gb[:, cols])
+            up = dot32(x2[top, own(0)], ua[:, cols]) + dot32(x2[top, own(1)], ub[:, cols])
+            act_ref[top, cols] = (jax.nn.silu(gate) * up).astype(jnp.bfloat16)
 
         def inner_step(n, carry):
             inner_block(block_at(n))
@@ -360,37 +356,94 @@
         if inner % WIDE:
             inner_block(pl.ds(whole * WIDE, inner % WIDE))
 
+    def down_part(slot):
+        y2 = y_ref.at[slot].reshape(tile, 2 * half)
+
         def down_step(n, carry):
             for side, weight in enumerate((da, db)):
-                y2[:, own_block(side, n)] = dot32(act_ref[...], weight[:, block_at(n)]).astype(jnp.bfloat16)
+                y2[:, own_block(side, n)] = dot32(act_ref[top, :], weight[:, block_at(n)]).astype(jnp.bfloat16)
             return carry
 
         lax.fori_loop(0, half // WIDE, down_step, 0)
 
-    fetch(go(0), 0)
-
-    def expert_unit(u):
-        slot = lax.rem(u, 2)
-        for copy in loads(go(u), slot):
+    def put(b, d, slot):
+        copies = [pltpu.make_async_copy(y_ref.at[slot, r], made_hbm.at[b * TURNS + r, d], y_sem.at[slot, r]) for r in range(TURNS)]
+        for copy in copies:
+            copy.start()
+        for copy in copies:
             copy.wait()
 
-        @pl.when(u + 1 < n_units)
-        def _():
-            fetch(go(u + 1), 1 - slot)
-
-        expert(slot)
-        copy = pltpu.make_async_copy(y_ref.at[slot], made_hbm.at[u], y_sem.at[slot])
-        copy.start()
-        copy.wait()
-        come(u).start(0)
-
-        @pl.when(u >= TURNS)
-        def _():
-            advance(come(u - TURNS), 0)
-
-    each(0, n_units, expert_unit)
-    each(n_units - TURNS, n_units, lambda u: advance(come(u), 0))
-    each(0, n_units, lambda u: advance(come(u), 1))
+    def near_tile(b):
+        copies = []
+        for r in range(TURNS):
+            for n, (src, place) in enumerate(go(b * TURNS + r).kept()):
+                copies.append(pltpu.make_async_copy(src, x_ref.at[(b, r, *place[1:])], x_sem.at[b, 3 * r + n]))
+        for copy in copies:
+            copy.start()
+        for copy in copies:
+            copy.wait()
+        inner_part(b)
+        down_part(b)
+        put(b, 0, b)
+
+    def far_of(s):
+        j = lax.rem(s, 3)
+        return s // 3, j, 1 + 2 * j - 3 * (j // 2)
+
+    def far_loads(s, slot):
+        b, _, d = far_of(s)
+        return [pltpu.make_async_copy(go(b * TURNS + r).last.at[d - 1], x_ref.at[slot, r], x_sem.at[slot, r]) for r in range(TURNS)]
+
+    def begin(s, slot):
+        b, _, d = far_of(s)
+        for r in range(TURNS):
+            go(b * TURNS + r).wait_last(d)
+        for copy in far_loads(s, slot):
+            copy.start()
+
+    def far_tile(s):
+        slot = lax.rem(s, 2)
+        b, j, d = far_of(s)
+
+        @pl.when(j == 0)
+        def _():
+            begin(s, slot)
+
+        for copy in far_loads(s, slot):
+            copy.wait()
+        inner_part(slot)
+
+        @pl.when(j < 2)
+        def _():
+            begin(s + 1, 1 - slot)
+
+        down_part(slot)
+        put(b, d, slot)
+        for r in range(TURNS):
+            come(b * TURNS + r).push(0, d)
+
+        @pl.when(s == 4)
+        def _():
+            each(0, TURNS, lambda u: advance(come(u), 0))
+
+    near_tile(0)
+    each(TURNS, n_units, lambda u: advance(go(u), 1))
+    near_tile(1)
+    each(0, n_units, far_tile)
+    each(0, TURNS, lambda u: advance(come(u), 1))
+    each(TURNS, n_units, lambda u: advance(come(u), 0))
+    each(TURNS, n_units, lambda u: advance(come(u), 1))
+
+    def loads(exchange, slot):
+        pieces = [(exchange.last, (pl.ds(1, 3),))] + exchange.kept()
+        return [pltpu.make_async_copy(src, x_ref.at[(slot, *place)], x_sem.at[slot, n]) for n, (src, place) in enumerate(pieces)]
+
+    def fetch(exchange, slot):
+        for d in range(1, RING):
+            exchange.wait_last(d)
+        for copy in loads(exchange, slot):
+            copy.start()
+
     fetch(come(0), 0)
 
     def mix(u):
@@ -429,9 +482,8 @@
     lax.fori_loop(0, n_shared, pair_done, 0)
 
     def sent(u):
-        for phase in range(3):
-            go(u).wait_send(phase)
-            come(u).wait_send(phase)
+        go(u).wait_sent()
+        come(u).wait_sent()
 
     each(0, n_units, sent)
 
@@ -461,12 +513,12 @@
             pltpu.VMEM((2, 2, WIDE, width // 2), jnp.bfloat16),
             pltpu.VMEM((2, *cube), jnp.bfloat16),
             pltpu.VMEM((RING ** 3 * BLOCK, inner), jnp.bfloat16),
-            pltpu.VMEM((2, *cube), jnp.bfloat16),
+            pltpu.VMEM((2, TURNS, *cube[1:]), jnp.bfloat16),
             pltpu.VMEM((n_tokens, width), jnp.float32),
             pltpu.VMEM((n_tokens, RING ** 3 * BLOCK), jnp.bfloat16),
             pltpu.VMEM((RING ** 3 * BLOCK, n_tokens), jnp.bfloat16),
-            sems((3,)), sems((3, n_shared)), sems((3, n_shared)), sems((3,)), sems((3,)), sems((2, 6)), sems((2, 4)), sems((2,)),
-            sems((n_units, 3)), sems((n_units, 3)), sems((n_units, 3)), sems((n_units, 3)),
+            sems((3,)), sems((3, n_shared)), sems((3, n_shared)), sems((3,)), sems((3,)), sems((2, 6)), sems((2, 9)), sems((2, 3)),
+            sems((n_units, 5)), sems((n_units, 5)), sems((n_units, 5)), sems((n_units, 5)),
         ],
         compiler_params=pltpu.CompilerParams(collective_id=0, has_side_effects=True, vmem_limit_bytes=60 * 1024 * 1024),
         cost_estimate=pl.CostEstimate(flops=250_000_000_000, bytes_accessed=100_000_000, transcendentals=0),

time: 378 us -> 359 us (0.950)
  Pallas kernels: 372 us -> 353 us
    pallas_call x1, Pallas kernels: 331 us -> 311 us  [moe_exchange(): pl.pallas_call(functools.partial(moe_kernel, n_units), out_shape=tuple(ou...]
where the time goes in v1:
time: 359 us; the launch traced here: 358 us
  Pallas kernels  353 us (98%)
    pallas_call x1, Pallas kernels, moe_exchange(): pl.pallas_call(functools.partial(moe_kernel, n_units), out_shape=tuple(ou...  311 us
    pallas_call x1, Pallas kernels, attention(): pl.pallas_call(attention_kernel, out_shape=(rows, rows), in_specs=[vmem]...  41.5 us

profile of v1, /device:TPU:0, one launch (start us, length us, event | category | flops | bytes accessed | tf_op | source)
XLA Modules:
  0.0 358.3 jit_solution(16565283854958643160)
XLA Ops:
  0.0 1.4 fusion.10.place_ref
  1.4 1.3 convert_bitcast_fusion.weight_ref
  2.7 41.5 %attention.1 = (bf16[384,2048]{1,0:T(8,128)(2,1)}, bf16[384,2048]{1,0:T(8,128)(2,1)}) custom-call(bf16[384,2048]{1,0:T(8,128)(2,1)} %bitcast.64, f32[384,128]{1,0:T(8,128)} %constant.110.clone.cos_ref, f32[384,128]{1,0:T(8,128)} %constant.111.clone.sin_ref, bf16[1024,6144]{1,0:T(8,128)(2,1)} %qkv_hbm.1, bf16[1024,2048]{1,0:T(8,128)(2,1)} %out_hbm.1), custom_call_target="tpu_custom_call" | custom-call | flops 20000000000 | bytes 40000000 | tf_op jit(solution)/shard_map/attention/pallas_call | solution.py:128
  44.2 311.4 %moe_exchange.1 = (bf16[384,2048]{1,0:T(8,128)(2,1)}, bf16[11,1024,256]{2,1,0:T(8,128)(2,1)}, bf16[11,1024,256]{2,1,0:T(8,128)(2,1)}, bf16[2816,1024]{1,0:T(8,12...) custom-call(bf16[384,2048]{1,0:T(8,128)(2,1)} %get-tuple-element.8.n, ...), custom_call_target="tpu_custom_call" | custom-call | flops 249999998976 | bytes 100000000 | tf_op jit(solution)/shard_map/moe_exchange/pallas_call | solution.py:506
  355.6 2.7 copy.62

commit v2 on v1

--- a/solution.py
+++ b/solution.py
@@ -72,35 +72,40 @@
     def own(side):
         return pl.ds(pl.multiple_of(lax.rem(fs + side, 2) * half, half), half)
 
-    def chunk_step(c, carry):
-        pltpu.make_async_copy(own_ref.at[c], own_ref.at[c], own_sem.at[c]).wait()
-        pltpu.make_async_copy(far_ref.at[c], far_ref.at[c], recv_sem.at[c]).wait()
+    def project(c):
         left, right = a_ref[:, own(0)], a_ref[:, own(1)]
-        q, k, v = [(dot32(left, own_ref[c, t]) + dot32(right, far_ref[c, t])).astype(jnp.bfloat16) for t in range(3)]
+        return [(dot32(left, own_ref[c, t]) + dot32(right, far_ref[c, t])).astype(jnp.bfloat16) for t in range(3)]
+
+    def chunk_step(pair, carry):
+        for c in (2 * pair, 2 * pair + 1):
+            pltpu.make_async_copy(own_ref.at[c], own_ref.at[c], own_sem.at[c]).wait()
+            pltpu.make_async_copy(far_ref.at[c], far_ref.at[c], recv_sem.at[c]).wait()
+        ready = [project(2 * pair + n) for n in range(2)]
 
         def rotate(vals):
             wide = vals.astype(jnp.float32)
             return (wide * cos_ref[...] + pltpu.roll(wide, HEAD_DIM // 2, 1) * sin_ref[...]).astype(jnp.bfloat16)
 
-        heads = []
-        for j in range(WIDE // HEAD_DIM):
-            cols = slice(j * HEAD_DIM, (j + 1) * HEAD_DIM)
-            query, key, value = rotate(q[:, cols]), rotate(k[:, cols]), v[:, cols]
-            parts = []
-            for i in range(seq_len // 128):
-                span = (i + 1) * 128
-                scores = lax.dot_general(query[i * 128:span], key[:span], (((1,), (1,)), ((), ())), preferred_element_type=jnp.float32) * (HEAD_DIM ** -0.5)
-                row_at = lax.broadcasted_iota(jnp.int32, (128, span), 0) + i * 128
-                col_at = lax.broadcasted_iota(jnp.int32, (128, span), 1)
-                scores = jnp.where(row_at >= col_at, scores, -1e30)
-                power = jnp.exp(scores - jnp.max(scores, axis=-1, keepdims=True))
-                probs = (power / jnp.sum(power, axis=-1, keepdims=True)).astype(jnp.bfloat16)
-                parts.append(dot32(probs, value[:span]).astype(jnp.bfloat16))
-            heads.append(jnp.concatenate(parts, axis=0))
-        o_ref[:, pl.ds(pl.multiple_of(c * WIDE, WIDE), WIDE)] = jnp.concatenate(heads, axis=1)
+        for n, (q, k, v) in enumerate(ready):
+            heads = []
+            for j in range(WIDE // HEAD_DIM):
+                cols = slice(j * HEAD_DIM, (j + 1) * HEAD_DIM)
+                query, key, value = rotate(q[:, cols]), rotate(k[:, cols]), v[:, cols]
+                parts = []
+                for i in range(seq_len // 128):
+                    span = (i + 1) * 128
+                    scores = lax.dot_general(query[i * 128:span], key[:span], (((1,), (1,)), ((), ())), preferred_element_type=jnp.float32) * (HEAD_DIM ** -0.5)
+                    row_at = lax.broadcasted_iota(jnp.int32, (128, span), 0) + i * 128
+                    col_at = lax.broadcasted_iota(jnp.int32, (128, span), 1)
+                    scores = jnp.where(row_at >= col_at, scores, -1e30)
+                    power = jnp.exp(scores - jnp.max(scores, axis=-1, keepdims=True))
+                    probs = (power / jnp.sum(power, axis=-1, keepdims=True)).astype(jnp.bfloat16)
+                    parts.append(dot32(probs, value[:span]).astype(jnp.bfloat16))
+                heads.append(jnp.concatenate(parts, axis=0))
+            o_ref[:, pl.ds(pl.multiple_of((2 * pair + n) * WIDE, WIDE), WIDE)] = jnp.concatenate(heads, axis=1)
         return carry
 
-    lax.fori_loop(0, n_chunks, chunk_step, 0)
+    lax.fori_loop(0, n_chunks // 2, chunk_step, 0)
     wo_load.wait()
     wo_push.wait_recv()
 
@@ -259,6 +264,14 @@
         for copy in shared_push(n):
             copy.start()
 
+    def pick_copy(u):
+        slot = lax.rem(u, 2)
+        return pltpu.make_async_copy(x_ref.at[slot], rows_hbm.at[u], y_sem.at[slot, 0])
+
+    def flush(u):
+        pick_copy(u).wait()
+        go(u).start(0)
+
     def pick(u):
         slot = lax.rem(u, 2)
         for c in range(rows // 128):
@@ -274,12 +287,14 @@
             return carry
 
         lax.fori_loop(0, 2 * half // WIDE, pick_step, 0)
-        copy = pltpu.make_async_copy(x_ref.at[slot], rows_hbm.at[u], y_sem.at[slot, 0])
-        copy.start()
-        copy.wait()
-        go(u).start(0)
+        @pl.when(u >= 1)
+        def _():
+            flush(u - 1)
+
+        pick_copy(u).start()
 
     each(0, n_units, pick)
+    flush(n_units - 1)
     weights = [pltpu.make_async_copy(src, dst, w_sem.at[n]) for n, (src, dst) in enumerate(((gate_a, ga), (up_a, ua), (down_a, da)))]
     far_weights = [pltpu.make_async_remote_copy(src_ref=src, dst_ref=dst, send_sem=far_send.at[n], recv_sem=far_recv.at[n], device_id=partner, device_id_type=MESH)
                    for n, (src, dst) in enumerate(((gate_a, gb), (up_a, ub), (down_a, db)))]

time: 359 us -> 355 us (0.989)
  no operation moved by 1% of the time
where the time goes in v2:
time: 355 us
  Pallas kernels  350 us (99%)
    pallas_call x1, Pallas kernels, moe_exchange(): pl.pallas_call(functools.partial(moe_kernel, n_units), out_shape=tuple(ou...  308 us
    pallas_call x1, Pallas kernels, attention(): pl.pallas_call(attention_kernel, out_shape=(rows, rows), in_specs=[vmem]...  41.4 us

profile of v2, /device:TPU:0, one launch (start us, length us, event | category | flops | bytes accessed | tf_op | source)
XLA Modules:
  0.0 355.0 jit_solution(3018864602664840480)
XLA Ops:
  0.0 1.4 fusion.10.place_ref
  1.4 1.3 convert_bitcast_fusion.weight_ref
  2.7 41.4 %attention.1 = (bf16[384,2048]{1,0:T(8,128)(2,1)}, bf16[384,2048]{1,0:T(8,128)(2,1)}) custom-call(bf16[384,2048]{1,0:T(8,128)(2,1)} %bitcast.64, f32[384,128]{1,0:T(8,128)} %constant.110.clone.cos_ref, f32[384,128]{1,0:T(8,128)} %constant.111.clone.sin_ref, bf16[1024,6144]{1,0:T(8,128)(2,1)} %qkv_hbm.1, bf16[1024,2048]{1,0:T(8,128)(2,1)} %out_hbm.1), custom_call_target="tpu_custom_call" | custom-call | flops 20000000000 | bytes 40000000 | tf_op jit(solution)/shard_map/attention/pallas_call | solution.py:133
  44.1 308.1 %moe_exchange.1 = (bf16[384,2048]{1,0:T(8,128)(2,1)}, bf16[11,1024,256]{2,1,0:T(8,128)(2,1)}, bf16[11,1024,256]{2,1,0:T(8,128)(2,1)}, bf16[2816,1024]{1,0:T(8,12...) custom-call(bf16[384,2048]{1,0:T(8,128)(2,1)} %get-tuple-element.8.n, ...), custom_call_target="tpu_custom_call" | custom-call | flops 249999998976 | bytes 100000000 | tf_op jit(solution)/shard_map/moe_exchange/pallas_call | solution.py:521
  352.2 2.7 copy.62
